TPU v7x, 256 devices: a whole 4x4x8 slice. The times are simulated.
256 devices in a mesh: row: 16 (over x, z_hi), col: 8 (over y, core), ga: 2 (over z_lo).
Axes of the slice: x: 4, y: 4, z: 8 (z_hi: 4, z_lo: 2; z = z_hi * 2 + z_lo), core: 2. Of those that a mesh axis runs over, the one named last changes fastest.
Arguments:
- pair_density: float32 [512, 24, 3072], P('row', None, 'ga'), may hold values from -6 to 6
- coulomb: float32 [3072], P('ga'), may hold values from 0.1 to 2
Outputs:
- kernel: float32 [12288, 12288], P('row', 'col')
All inputs are finite; a program needn't handle non-finite values.
Results may differ from a plain program's by a relative error of at most 0.00011.
Values sent between devices are 32-bit elements; how exact they have to be, the bound alone decides.
A program may use at most 64 MiB of HBM per device.

v0:
```python
import jax
import jax.numpy as jnp
from jax import lax
from jax.sharding import PartitionSpec as P


def rows_for(lines, peers):
    spare = -lines.shape[0] % peers
    if not spare:
        return lines
    return jnp.concatenate([lines, jnp.zeros((spare, *lines.shape[1:]), lines.dtype)])


def from_root(value, axis, root):
    lines = jnp.where(lax.axis_index(axis) == root, value, jnp.zeros_like(value)).reshape(
        -1, *value.shape[1:][-1:]
    )
    padded = rows_for(lines, lax.axis_size(axis))
    own = lax.psum_scatter(padded, axis, scatter_dimension=0, tiled=True)
    return lax.all_gather(own, axis, axis=0, tiled=True)[: len(lines)].reshape(value.shape)


def sent_to_all(value, axis):
    copies = jnp.broadcast_to(value, (lax.axis_size(axis), *value.shape))
    return lax.all_to_all(copies, axis, split_axis=0, concat_axis=0, tiled=True)


def taken_together(value, axis):
    return sent_to_all(value, axis).sum(axis=0)


def contract(left_rows, right_rows):
    return lax.dot_general(
        left_rows,
        right_rows,
        (((1,), (1,)), ((), ())),
        precision=lax.Precision.HIGHEST,
        preferred_element_type=jnp.float32,
    )


def local(pair_density, coulomb):
    row_count = lax.axis_size("row")
    col_count = lax.axis_size("col")
    here_row = lax.axis_index("row")
    here_col = lax.axis_index("col")
    doubled = 2.0 * coulomb
    local_k, bands, g_width = pair_density.shape
    grouped = pair_density.reshape(local_k // col_count, col_count, bands, g_width)
    own_columns = lax.dynamic_index_in_dim(grouped, here_col, 1, keepdims=False)
    columns = lax.all_gather(own_columns, "row", axis=0, tiled=True)
    ratio = row_count // col_count
    chosen = lax.dynamic_index_in_dim(
        columns.reshape(local_k, ratio, bands, g_width), here_row // col_count, 1, keepdims=False
    )
    rows_data = from_root(chosen, "col", here_row % col_count)
    weighted = rows_data.reshape(local_k * bands, g_width) * doubled[None, :]
    partial_value = contract(weighted, columns.reshape(columns.shape[0] * bands, g_width))
    summed = taken_together(partial_value, "ga")
    total_k = local_k * row_count
    return summed / jnp.float32(total_k)


def solution(mesh):
    placed = (P("row", None, "ga"), P("ga"))
    return jax.shard_map(
        local, mesh=mesh, in_specs=placed, out_specs=P("row", "col"), check_vma=False
    )
```

profile of v0, /device:TPU:16, one launch (start us, length us, event | category | flops | bytes accessed | tf_op | source)
XLA Modules:
  0.0 378.7 jit_solution(15559402277794939784)
XLA Ops:
  6.5 0.0 all-gather.6.cloned.1.call-start
  6.5 1.9 constant_dynamic-slice_fusion
  8.5 0.0 all-gather.6.cloned.1.call-update
  8.5 0.0 reduce-scatter.2.cloned.1.call-start
  8.6 125.1 %all-gather.6.cloned.1.call-done = f32[64,1,24,1536]{3,2,1,0:T(8,128)} async-done(((f32[4,1,24,1536]{3,2,1,0:T(8,128)}), f32[64,1,24,1536]{3,2,1,0:T(8,128)}) %all-gather.6.cloned.1.call-update) | async-done | bytes 9437200 | tf_op jit(solution)/shard_map/all_gather | solution.py:51
  133.7 5.0 %dynamic-slice_select_fusion = f32[32,1,24,1536]{3,2,1,0:T(8,128)} fusion(f32[32,2,24,1536]{3,2,1,0:T(8,128)} %bitcast.6, s32[]{:T(128)S(6)} %select_n.35, pred[]{:T(512)S(6)} %eq.5), kind=kLoop, calls=%fused_computation.2 | loop fusion | flops 1179648 | bytes 9437189 | tf_op jit(solution)/shard_map/jit(_where)/select_n | solution.py:15
  138.6 0.0 copy-start
  138.6 0.0 reduce-scatter.2.cloned.1.call-update
  138.7 0.0 all-gather.4.cloned.1.call-start
  138.7 42.3 %reduce-scatter.2.cloned.1.call-done = f32[96,1536]{1,0:T(8,128)} async-done(((f32[768,1536]{1,0:T(8,128)}), f32[96,1536]{1,0:T(8,128)}) %reduce-scatter.2.cloned.1.call-update) | async-done | bytes 589840 | tf_op jit(solution)/shard_map/reduce_scatter | solution.py:19
  181.0 0.0 all-gather.4.cloned.1.call-update
  181.0 0.0 copy-done
  181.0 40.9 %all-gather.4.cloned.1.call-done = f32[768,1536]{1,0:T(8,128)} async-done(((f32[96,1536]{1,0:T(8,128)}), f32[768,1536]{1,0:T(8,128)}) %all-gather.4.cloned.1.call-update) | async-done | bytes 4718608 | tf_op jit(solution)/shard_map/all_gather | solution.py:20
  222.0 28.0 %fusion = f32[768,1536]{1,0:T(8,128)S(1)} fusion(f32[1536,1536]{1,0:T(8,128)} %bitcast.7, f32[768,1536]{1,0:T(8,128)} %all-gather.4.cloned.1.call-done, f32[1536]{0:T(1024)S(1)} %broadcast_multiply_fusion.1), kind=kOutput, calls=%fused_computation | convolution fusion | flops 21744451584 | bytes 18880512 | tf_op jit(solution)/shard_map/dot_general | solution.py:33
  250.0 1.2 broadcast_in_dim.8
  251.2 108.7 %all_to_all.5 = f32[2,768,1536]{2,1,0:T(8,128)} all-to-all(f32[2,768,1536]{2,1,0:T(8,128)S(1)} %broadcast_in_dim.8), channel_id=1, replica_groups=mesh['row'=16,'col'=8,'ga'=2] {'ga'}, dimensions={0} | all-to-all | bytes 18874368 | tf_op jit(solution)/shard_map/all_to_all | solution.py:25
  359.9 7.3 %reduce_sum.9 = f32[768,1536]{1,0:T(8,128)} reduce(f32[2,768,1536]{2,1,0:T(8,128)} %all_to_all.5, f32[]{:T(128)} %constant.51.clone.1), dimensions={0}, to_apply=%region_1.2 | reduce | flops 1179648 | bytes 14155780 | tf_op jit(solution)/shard_map/reduce_sum | solution.py:29
  367.2 5.0 %broadcast_multiply_fusion = f32[768,1536]{1,0:T(8,128)} fusion(f32[768,1536]{1,0:T(8,128)} %reduce_sum.9), kind=kLoop, calls=%fused_computation.3 | loop fusion | flops 1179648 | bytes 9437184 | tf_op jit(solution)/shard_map/div | solution.py:61
  (1 shorter events, 0.0 us)
Async XLA Ops:
  6.5 127.1 %all-gather.6.cloned.1.call-start = ((), (), s32[]{:S(2)}) async-start(), calls=%async_computation.4 | async-start | bytes 10027008 | tf_op jit(solution)/shard_map/all_gather | solution.py:51
  8.5 172.5 %reduce-scatter.2.cloned.1.call-start = ((), (), s32[]{:S(2)}) async-start(), calls=%async_computation.2 | async-start | bytes 5308416 | tf_op jit(solution)/shard_map/reduce_scatter | solution.py:19
  138.6 42.4 %copy-start = (f32[1536]{0:T(1024)S(1)}, f32[1536]{0:T(1024)}, u32[]{:S(2)}) copy-start(f32[1536]{0:T(1024)} %param.3) | copy-start | bytes 18436
  138.7 83.3 %all-gather.4.cloned.1.call-start = ((), (), s32[]{:S(2)}) async-start(), calls=%async_computation.3 | async-start | bytes 5308416 | tf_op jit(solution)/shard_map/all_gather | solution.py:20
Sparse Core Ops, SparseCore 0:
  9.8 123.8 all-gather.5
  138.8 42.1 reduce-scatter.1
  182.8 39.0 all-gather.3
where the time goes:
time: 381 us; the launch traced here: 379 us
  waiting for transfers between devices  208 us (55%)
  blocking collectives  109 us (29%)
  matrix products  28 us (7%)
  other arithmetic  17.3 us (5%)
  between operations  13.2 us (3%)
    all_gather x1, waiting for transfers between devices, local(): columns = lax.all_gather(own_columns, 'row', axis=0, tiled=True)  125 us
    all_to_all x1, blocking collectives, sent_to_all(): return lax.all_to_all(copies, axis, split_axis=0, concat_axis=0, tiled=True)  109 us
    reduce_scatter x1, waiting for transfers between devices, from_root(): own = lax.psum_scatter(padded, axis, scatter_dimension=0, tiled=True)  42.3 us
    all_gather x1, waiting for transfers between devices, from_root(): lax.all_gather(own, axis, axis=0, tiled=True)[:len(lines)]  40.9 us
    dot_general x1, matrix products, contract(): lax.dot_general(left_rows, right_rows, (((1,), (1,)), ((), ())), precisio...  28 us
  transfers between devices with their start and end apart: 3, of which 3 were waited for; matrix products, arithmetic and copies ran while one was open for 0% of the time, Pallas kernels for 0%

commit v1 on v0

v1 whole, which is shorter than its diff:
```python
import jax
import jax.numpy as jnp
from jax import lax
from jax.experimental import pallas as pl
from jax.experimental.pallas import tpu as pltpu
from jax.sharding import PartitionSpec as P

MESH = pl.DeviceIdType.MESH
F32 = jnp.float32
BF16 = jnp.bfloat16

LAG = 2
PLAN = (
    (0, 0, -1, -1),
    (2, 2, -1, -1),
    (3, 3, 2, 1),
    (1, 1, 1, 3),
    (30, 30, 3, 5),
    (96, 7, 0, 0),
    (7, 31, 31, 7),
    (4, 4, 30, 4),
    (28, 28, 28, 9),
    (31, 29, 29, 2),
    (8, 8, 26, 11),
    (6, 6, 24, 6),
    (24, 24, 27, 8),
    (98, 5, 25, 10),
    (29, 10, 23, 12),
    (5, 26, 21, 14),
    (26, 35, 61, 37),
    (10, 11, 63, 101),
    (100, 60, 57, 41),
    (97, 12, 59, 43),
    (27, 20, 53, 105),
    (11, 62, 55, 42),
    (25, 38, 123, 109),
    (20, 22, 122, 107),
    (12, 39, 121, 46),
    (14, 63, 52, 111),
    (104, 56, 118, 65),
    (16, 58, 65, 71),
    (106, 59, 88, 69),
    (108, 57, 90, 75),
    (110, 48, 91, 73),
    (113, 50, 89, 79),
)
STEPS = ((1, 0), (-1, 0), (0, 1), (0, -1))
NX, NZ, NY = 4, 8, 4
GROUP_ORDER = (0, 1, 3, 2)
M_TILE = 256

AT_ROWS, AT_PAIR, AT_FIRST, AT_SECOND, AT_RELAY, AT_CORE = 5, 8, 10, 14, 18, 20
UNITS = {21: 1, 22: 1, 23: 1, 24: 1, 25: 1, 26: 1, 27: 3, 28: 3, 29: 2, 30: 2, 31: 2}


def split(value):
    high = value.astype(BF16)
    return high, (value - high.astype(F32)).astype(BF16)


def contract(left, right):
    return lax.dot_general(
        left, right, (((1,), (1,)), ((), ())), preferred_element_type=F32
    )


def kernel(
    pairs, scale, out,
    cols, rows, scales, left_hi, left_lo, right_hi, right_lo, total,
    col_send, col_recv, row_send, row_recv, sub_send, sub_recv, own_sem, out_sem,
):
    row, col, half = lax.axis_index("row"), lax.axis_index("col"), lax.axis_index("ga")
    x, y, core = row // 4, col // 2, col % 2
    z = 2 * (row % 4) + half
    other = 1 - half
    width = pairs.shape[2]
    quarter = width // NY
    bands = pairs.shape[1]
    n_row = 16

    def place(xx, zz, cc=None):
        return {"row": 4 * xx + zz // 2, "col": col if cc is None else cc, "ga": zz % 2}

    def near(step):
        return place((x + step[0] + NX) % NX, (z + step[1] + NZ) % NZ)

    y_up = {"row": row, "col": (col + 2) % 8, "ga": half}
    y_down = {"row": row, "col": (col + 6) % 8, "ga": half}
    twin = {"row": row, "col": 2 * y + 1 - core, "ga": half}
    pair = {"row": row, "col": col, "ga": other}
    z_out = near((0, 1)), near((0, -1))

    def remote(src, dst, send, recv, device):
        return pltpu.make_async_remote_copy(
            src_ref=src, dst_ref=dst, send_sem=send, recv_sem=recv,
            device_id=device, device_id_type=MESH,
        )

    barrier = pltpu.get_barrier_semaphore()
    for step in range(1, n_row):
        pl.semaphore_signal(
            barrier, inc=1, device_id={"row": (row + step) % n_row, "col": col, "ga": half},
            device_id_type=MESH,
        )
    for device in (*z_out, y_up, y_down, twin):
        pl.semaphore_signal(barrier, inc=1, device_id=device, device_id_type=MESH)

    lanes = pl.ds(pl.multiple_of(y * quarter, 128), quarter)
    own_rows = pltpu.make_async_copy(
        pairs.at[row + 16 * core, :, lanes], rows.at[half, y, core, row], own_sem.at[0]
    )
    own_rows.start()
    own_scale = pltpu.make_async_copy(scale, scales.at[half], own_sem.at[1])
    own_scale.start()
    own_cols = []
    for piece in range(4):
        own_cols.append(pltpu.make_async_copy(
            pairs.at[col + 8 * piece], cols.at[half, 4 * row + piece], own_sem.at[2 + piece]
        ))
        own_cols[-1].start()

    pl.semaphore_wait(barrier, n_row - 1 + 5)

    sends = []

    def go(copy):
        copy.start()
        sends.append(copy)

    go(remote(scale, scales.at[half], sub_send.at[0], sub_recv.at[0], pair))
    for step in range(1, n_row):
        to = (row + step) % n_row
        go(remote(
            pairs.at[to + 16 * core, :, lanes], rows.at[half, y, core, row],
            row_send.at[step], row_recv.at[step], {"row": to, "col": col, "ga": half},
        ))

    def slot(code, step=(0, 0)):
        xs = (x + code // 32 - step[0] + NX) % NX
        zs = (z + (code // 4) % 8 - step[1] + NZ) % NZ
        return zs % 2, 4 * (4 * xs + zs // 2) + code % 4

    def send_round(number):
        for way, code in enumerate(PLAN[number]):
            if code < 0:
                continue
            where = cols.at[slot(code)]
            src = pairs.at[col + 8 * (code % 4)] if code < 4 else where
            index = 4 * number + way
            go(remote(src, where, col_send.at[index], col_recv.at[index], near(STEPS[way])))

    def wait_round(number):
        for way, code in enumerate(PLAN[number]):
            if code < 0:
                continue
            where = cols.at[slot(code, STEPS[way])]
            index = 4 * number + way
            remote(
                where, where, col_send.at[index], col_recv.at[index], near(STEPS[way])
            ).wait_recv()

    def part(h, yy, cc):
        return rows.at[h, (yy + NY) % NY, cc]

    def send_part(h, yy, number, device):
        ref = part(h, yy, core)
        go(remote(ref, ref, sub_send.at[number], sub_recv.at[number], device))

    def wait_part(h, yy, cc, number):
        ref = part(h, yy, cc)
        remote(ref, ref, sub_send.at[number], sub_recv.at[number], twin).wait_recv()

    def to_twin(h, yy, number):
        send_part(h, yy, number, twin)

    def exchange(number):
        if number == AT_ROWS:
            own_rows.wait()
            for step in range(1, n_row):
                where = rows.at[half, y, core, (row + n_row - step) % n_row]
                remote(
                    where, where, row_send.at[step], row_recv.at[step], pair
                ).wait_recv()
            send_part(half, y, 1, pair)
            send_part(half, y, 2, y_up)
            send_part(half, y, 3, y_down)
            to_twin(half, y, 8)
        if number == AT_PAIR:
            wait_part(other, y, core, 1)
            send_part(other, y, 4, y_up)
            send_part(other, y, 5, y_down)
            to_twin(other, y, 9)
        if number == AT_FIRST:
            wait_part(half, y - 1, core, 2)
            send_part(half, y - 1, 6, y_up)
            to_twin(half, y - 1, 10)
            wait_part(half, y + 1, core, 3)
            to_twin(half, y + 1, 11)
        if number == AT_SECOND:
            wait_part(other, y + 1, core, 5)
            send_part(other, y + 1, 7, y_down)
            to_twin(other, y + 1, 12)
            wait_part(other, y - 1, core, 4)
            to_twin(other, y - 1, 13)
        if number == AT_RELAY:
            wait_part(half, y - 2, core, 6)
            to_twin(half, y - 2, 14)
            wait_part(other, y + 2, core, 7)
            to_twin(other, y + 2, 15)
        if number == AT_CORE:
            own_scale.wait()
            remote(scale, scales.at[other], sub_send.at[0], sub_recv.at[0], pair).wait_recv()
            for n, (h, yy) in enumerate((
                (half, y), (other, y), (half, y - 1), (half, y + 1),
                (other, y + 1), (other, y - 1), (half, y - 2), (other, y + 2),
            )):
                wait_part(h, yy, 1 - core, 8 + n)

            def fill(i, carry):
                h, yy, r = i // (NY * n_row), (i // n_row) % NY, i % n_row
                at = pl.ds(pl.multiple_of(yy * quarter, 128), quarter)
                both = jnp.concatenate([rows[h, yy, 0, r], rows[h, yy, 1, r]], axis=0)
                hi, lo = split(both * scales[h, 0:1, at])
                to = pl.ds(pl.multiple_of(r * 2 * bands, 16), 2 * bands)
                left_hi[h, to, at] = hi
                left_lo[h, to, at] = lo
                return carry

            lax.fori_loop(0, 2 * NY * n_row, fill, 0)

    def unit(u, carry):
        group, part_no, tile = u // 6, (u // 3) % 2, u % 3
        ox = group + (group // 2) * (5 - 2 * group)
        xs = (x + ox) % NX
        h = (half + part_no) % 2

        @pl.when(tile == 0)
        def _():
            def fill(i, c):
                block = cols[h, pl.ds(16 * xs + 2 * i, 2)].reshape(2 * bands, width)
                hi, lo = split(block)
                to = pl.ds(pl.multiple_of(i * 2 * bands, 16), 2 * bands)
                right_hi[to, :] = hi
                right_lo[to, :] = lo
                return c

            lax.fori_loop(0, 8, fill, 0)

        m = pl.ds(pl.multiple_of(tile * M_TILE, M_TILE), M_TILE)
        hi, lo = right_hi[...], right_lo[...]
        result = contract(left_hi[h, m, :], hi)
        result += contract(left_hi[h, m, :], lo)
        result += contract(left_lo[h, m, :], hi)

        @pl.when(part_no == 0)
        def _():
            total[group, m, :] = result

        @pl.when(part_no == 1)
        def _():
            total[group, m, :] += result
            at = pl.ds(pl.multiple_of(xs * 16 * bands, 128), 16 * bands)
            pltpu.make_async_copy(
                total.at[group, m, :], out.at[m, at], out_sem.at[3 * group + tile]
            ).start()

        return carry

    rounds = len(PLAN)
    done = 0
    for number in range(rounds):
        if number >= LAG:
            wait_round(number - LAG)
        send_round(number)
        exchange(number)
        count = UNITS.get(number, 0)
        if count:
            if done == 0:
                for copy in own_cols:
                    copy.wait()
            lax.fori_loop(done, done + count, unit, 0)
            done += count
    for number in range(rounds - LAG, rounds):
        wait_round(number)
    lax.fori_loop(done, 24, unit, 0)

    def flush(u, carry):
        group, tile = u // 3, u % 3
        ox = group + (group // 2) * (5 - 2 * group)
        xs = (x + ox) % NX
        m = pl.ds(pl.multiple_of(tile * M_TILE, M_TILE), M_TILE)
        at = pl.ds(pl.multiple_of(xs * 16 * bands, 128), 16 * bands)
        pltpu.make_async_copy(
            total.at[group, m, :], out.at[m, at], out_sem.at[3 * group + tile]
        ).wait()
        return carry

    for copy in sends:
        copy.wait_send()
    lax.fori_loop(0, 12, flush, 0)


def local(pair_density, coulomb):
    local_k, bands, width = pair_density.shape
    n_row = lax.axis_size("row")
    total_k = local_k * n_row
    scale = jnp.broadcast_to((2.0 * coulomb / F32(total_k))[None, :], (8, width))
    m = 2 * n_row * bands
    n = 4 * n_row * bands
    group = n // NX
    rounds = len(PLAN)
    return pl.pallas_call(
        kernel,
        out_shape=jax.ShapeDtypeStruct((m, n), F32),
        in_specs=[pl.BlockSpec(memory_space=pl.ANY), pl.BlockSpec(memory_space=pltpu.VMEM)],
        out_specs=pl.BlockSpec(memory_space=pl.ANY),
        scratch_shapes=[
            pltpu.VMEM((2, 4 * n_row, bands, width), F32),
            pltpu.VMEM((2, NY, 2, n_row, bands, width // NY), F32),
            pltpu.VMEM((2, 8, width), F32),
            pltpu.VMEM((2, m, width), BF16),
            pltpu.VMEM((2, m, width), BF16),
            pltpu.VMEM((group, width), BF16),
            pltpu.VMEM((group, width), BF16),
            pltpu.VMEM((NX, m, group), F32),
            pltpu.SemaphoreType.DMA((4 * rounds,)),
            pltpu.SemaphoreType.DMA((4 * rounds,)),
            pltpu.SemaphoreType.DMA((n_row,)),
            pltpu.SemaphoreType.DMA((n_row,)),
            pltpu.SemaphoreType.DMA((16,)),
            pltpu.SemaphoreType.DMA((16,)),
            pltpu.SemaphoreType.DMA((6,)),
            pltpu.SemaphoreType.DMA((12,)),
        ],
        compiler_params=pltpu.CompilerParams(
            collective_id=0, has_side_effects=True, vmem_limit_bytes=64 * 1024 * 1024 - 2 * 1024 * 1024
        ),
        name="gather_and_contract",
    )(pair_density, scale)


def solution(mesh):
    placed = (P("row", None, "ga"), P("ga"))
    return jax.shard_map(
        local, mesh=mesh, in_specs=placed, out_specs=P("row", "col"), check_vma=False
    )
```

time: 381 us -> 156 us (0.41)
  waiting for transfers between devices: 208 us -> 0 us
  Pallas kernels: 0 us -> 150 us
  blocking collectives: 109 us -> 0 us
  matrix products: 28 us -> 0 us
  other arithmetic: 17.3 us -> 0.7 us
  between operations: 13.2 us -> 0.01 us
    all_gather x2 -> x0, waiting for transfers between devices: 166 us -> none  [the longest x1 125 us: local(): columns = lax.all_gather(own_columns, 'row', axis=0, tiled=True)]
    pallas_call x0 -> x1, Pallas kernels: none -> 150 us  [local(): pl.pallas_call(kernel, out_shape=jax.ShapeDtypeStruct((m, n), F32), in_sp...]
    all_to_all x1 -> x0, blocking collectives: 109 us -> none  [sent_to_all(): return lax.all_to_all(copies, axis, split_axis=0, concat_axis=0, tiled=True)]
    reduce_scatter x1 -> x0, waiting for transfers between devices: 42.3 us -> none  [from_root(): own = lax.psum_scatter(padded, axis, scatter_dimension=0, tiled=True)]
    dot_general x1 -> x0, matrix products: 28 us -> none  [contract(): lax.dot_general(left_rows, right_rows, (((1,), (1,)), ((), ())), precisio...]
    reduce_sum x1 -> x0, other arithmetic: 7.29 us -> none  [taken_together(): return sent_to_all(value, axis).sum(axis=0)]
    select_n x1 -> x0, other arithmetic: 4.98 us -> none  [from_root(): jnp.where(lax.axis_index(axis) == root, value, jnp.zeros_like(value))]
    unnamed x2 -> x1, local copies, waits for them, and re-layouts: 0.01 us -> 4.84 us
  transfers between devices with their start and end apart: 3 -> 0, of which waited for: 3 -> 0; matrix products, arithmetic and copies ran while one was open for 0% -> 0% of each run, Pallas kernels for 0% -> 0%
where the time goes in v1:
time: 156 us
  Pallas kernels  150 us (96%)
  local copies, waits for them, and re-layouts  5.47 us (4%)
    pallas_call x1, Pallas kernels, local(): pl.pallas_call(kernel, out_shape=jax.ShapeDtypeStruct((m, n), F32), in_sp...  150 us
    unnamed x1, local copies, waits for them, and re-layouts  4.84 us

profile of v1, /device:TPU:16, one launch (start us, length us, event | category | flops | bytes accessed | tf_op | source)
XLA Modules:
  0.0 156.2 jit_solution(9112996038316798705)
XLA Ops:
  0.0 0.7 broadcast_multiply_fusion
  0.7 0.6 broadcast_in_dim.2.scale
  1.3 150.1 %gather_and_contract.1 = f32[768,1536]{1,0:T(8,128)} custom-call(f32[32,24,1536]{2,1,0:T(8,128)} %pairs.1, f32[8,1536]{1,0:T(8,128)} %broadcast_in_dim.2.scale), custom_call_target="tpu_custom_call" | custom-call | tf_op jit(solution)/shard_map/gather_and_contract/pallas_call | solution.py:312
  151.4 4.8 %copy.4 = f32[768,1536]{1,0:T(8,128)} copy(f32[768,1536]{1,0:T(8,128)} %gather_and_contract.1) | data formatting | bytes 9437184

commit v2 on v1

--- a/solution.py
+++ b/solution.py
@@ -9,48 +9,57 @@
 F32 = jnp.float32
 BF16 = jnp.bfloat16
 
-LAG = 2
+LAG = 3
 PLAN = (
-    (0, 0, -1, -1),
     (2, 2, -1, -1),
-    (3, 3, 2, 1),
-    (1, 1, 1, 3),
-    (30, 30, 3, 5),
-    (96, 7, 0, 0),
-    (7, 31, 31, 7),
-    (4, 4, 30, 4),
-    (28, 28, 28, 9),
-    (31, 29, 29, 2),
-    (8, 8, 26, 11),
-    (6, 6, 24, 6),
-    (24, 24, 27, 8),
-    (98, 5, 25, 10),
-    (29, 10, 23, 12),
-    (5, 26, 21, 14),
-    (26, 35, 61, 37),
-    (10, 11, 63, 101),
-    (100, 60, 57, 41),
-    (97, 12, 59, 43),
-    (27, 20, 53, 105),
-    (11, 62, 55, 42),
-    (25, 38, 123, 109),
-    (20, 22, 122, 107),
-    (12, 39, 121, 46),
-    (14, 63, 52, 111),
-    (104, 56, 118, 65),
-    (16, 58, 65, 71),
-    (106, 59, 88, 69),
-    (108, 57, 90, 75),
-    (110, 48, 91, 73),
-    (113, 50, 89, 79),
+    (1, 1, -1, -1),
+    (3, 0, -1, -1),
+    (0, 3, 3, 2),
+    (97, 34, 0, 3),
+    (99, 32, 2, 1),
+    (6, 6, 1, 0),
+    (28, 7, 28, 6),
+    (30, 30, 30, 5),
+    (5, 29, 31, 7),
+    (10, 10, 29, 4),
+    (26, 26, 35, 32),
+    (9, 9, 32, 33),
+    (25, 25, 26, 99),
+    (24, 24, 99, 11),
+    (8, 27, 25, 9),
+    (22, 22, 27, 10),
+    (15, 15, 24, 8),
+    (21, 21, 104, 121),
+    (14, 14, 21, 39),
+    (13, 13, 111, 36),
+    (20, 23, 127, 14),
+    (17, 17, 20, 15),
+    (12, 54, 56, 40),
+    (18, 18, 123, 47),
+    (16, 16, 67, 67),
+    (19, 46, 64, 64),
+    (106, 50, 65, 65),
+    (122, 49, 66, 66),
+    (112, 45, 95, 71),
+    (116, 53, 92, 68),
+    (108, 51, 93, 69),
+    (119, -1, -1, 75),
 )
 STEPS = ((1, 0), (-1, 0), (0, 1), (0, -1))
 NX, NZ, NY = 4, 8, 4
-GROUP_ORDER = (0, 1, 3, 2)
 M_TILE = 256
+FIRST_LIMIT, LAST_LIMIT = 36 * 2**20, 6 * 2**20
 
 AT_ROWS, AT_PAIR, AT_FIRST, AT_SECOND, AT_RELAY, AT_CORE = 5, 8, 10, 14, 18, 20
-UNITS = {21: 1, 22: 1, 23: 1, 24: 1, 25: 1, 26: 1, 27: 3, 28: 3, 29: 2, 30: 2, 31: 2}
+PARTS = ((0, 1), (0, 0), (1, 1), (3, 1), (1, 0), (3, 0), (2, 0), (2, 1))
+OPENS = (1, 0, 1, 1, 0, 0, 1, 0)
+TILES = {21: 1, 22: 1, 23: 1, 25: 2, 26: 2, 27: 2, 28: 2, 29: 2, 30: 2, 31: 2, 32: 1}
+EARLY = 21
+N_TILE = 3
+
+
+def pick(table, index):
+    return sum(jnp.where(index == k, v, 0) for k, v in enumerate(table))
 
 
 def split(value):
@@ -64,10 +73,30 @@
     )
 
 
+def three(left_hi, left_lo, right_hi, right_lo):
+    result = contract(left_hi, right_hi)
+    result += contract(left_hi, right_lo)
+    result += contract(left_lo, right_hi)
+    return result
+
+
+def fill_right(cols, right_hi, right_lo, h, xs):
+    bands, width = cols.shape[2:]
+
+    def fill(i, carry):
+        hi, lo = split(cols[h, pl.ds(16 * xs + 2 * i, 2)].reshape(2 * bands, width))
+        to = pl.ds(pl.multiple_of(i * 2 * bands, 16), 2 * bands)
+        right_hi[to, :] = hi
+        right_lo[to, :] = lo
+        return carry
+
+    lax.fori_loop(0, 8, fill, 0)
+
+
 def kernel(
-    pairs, scale, out,
-    cols, rows, scales, left_hi, left_lo, right_hi, right_lo, total,
-    col_send, col_recv, row_send, row_recv, sub_send, sub_recv, own_sem, out_sem,
+    pairs, coulomb, left_hi, left_lo, right_hi, right_lo, total,
+    cols, rows, scales,
+    col_send, col_recv, row_send, row_recv, sub_send, sub_recv, own_sem,
 ):
     row, col, half = lax.axis_index("row"), lax.axis_index("col"), lax.axis_index("ga")
     x, y, core = row // 4, col // 2, col % 2
@@ -110,8 +139,8 @@
         pairs.at[row + 16 * core, :, lanes], rows.at[half, y, core, row], own_sem.at[0]
     )
     own_rows.start()
-    own_scale = pltpu.make_async_copy(scale, scales.at[half], own_sem.at[1])
-    own_scale.start()
+    per_row = 2.0 * coulomb[...].reshape(1, width) / F32(pairs.shape[0] * n_row)
+    scales[half] = jnp.broadcast_to(per_row, (8, width))
     own_cols = []
     for piece in range(4):
         own_cols.append(pltpu.make_async_copy(
@@ -127,7 +156,6 @@
         copy.start()
         sends.append(copy)
 
-    go(remote(scale, scales.at[half], sub_send.at[0], sub_recv.at[0], pair))
     for step in range(1, n_row):
         to = (row + step) % n_row
         go(remote(
@@ -181,6 +209,9 @@
                 remote(
                     where, where, row_send.at[step], row_recv.at[step], pair
                 ).wait_recv()
+            go(remote(
+                scales.at[half], scales.at[half], sub_send.at[0], sub_recv.at[0], pair
+            ))
             send_part(half, y, 1, pair)
             send_part(half, y, 2, y_up)
             send_part(half, y, 3, y_down)
@@ -208,8 +239,9 @@
             wait_part(other, y + 2, core, 7)
             to_twin(other, y + 2, 15)
         if number == AT_CORE:
-            own_scale.wait()
-            remote(scale, scales.at[other], sub_send.at[0], sub_recv.at[0], pair).wait_recv()
+            remote(
+                scales.at[other], scales.at[other], sub_send.at[0], sub_recv.at[0], pair
+            ).wait_recv()
             for n, (h, yy) in enumerate((
                 (half, y), (other, y), (half, y - 1), (half, y + 1),
                 (other, y + 1), (other, y - 1), (half, y - 2), (other, y + 2),
@@ -228,41 +260,26 @@
 
             lax.fori_loop(0, 2 * NY * n_row, fill, 0)
 
-    def unit(u, carry):
-        group, part_no, tile = u // 6, (u // 3) % 2, u % 3
-        ox = group + (group // 2) * (5 - 2 * group)
-        xs = (x + ox) % NX
-        h = (half + part_no) % 2
-
-        @pl.when(tile == 0)
+    def tile(u, carry):
+        number, m_tile = u // N_TILE, u % N_TILE
+        xs = (x + pick([ox for ox, _ in PARTS], number)) % NX
+        h = (half + pick([oz for _, oz in PARTS], number)) % 2
+
+        @pl.when(m_tile == 0)
         def _():
-            def fill(i, c):
-                block = cols[h, pl.ds(16 * xs + 2 * i, 2)].reshape(2 * bands, width)
-                hi, lo = split(block)
-                to = pl.ds(pl.multiple_of(i * 2 * bands, 16), 2 * bands)
-                right_hi[to, :] = hi
-                right_lo[to, :] = lo
-                return c
-
-            lax.fori_loop(0, 8, fill, 0)
-
-        m = pl.ds(pl.multiple_of(tile * M_TILE, M_TILE), M_TILE)
-        hi, lo = right_hi[...], right_lo[...]
-        result = contract(left_hi[h, m, :], hi)
-        result += contract(left_hi[h, m, :], lo)
-        result += contract(left_lo[h, m, :], hi)
-
-        @pl.when(part_no == 0)
+            fill_right(cols, right_hi, right_lo, h, xs)
+
+        m = pl.ds(pl.multiple_of(m_tile * M_TILE, M_TILE), M_TILE)
+        result = three(left_hi[h, m, :], left_lo[h, m, :], right_hi[...], right_lo[...])
+        opens = pick(OPENS, number)
+
+        @pl.when(opens == 1)
         def _():
-            total[group, m, :] = result
-
-        @pl.when(part_no == 1)
+            total[xs, m, :] = result
+
+        @pl.when(opens == 0)
         def _():
-            total[group, m, :] += result
-            at = pl.ds(pl.multiple_of(xs * 16 * bands, 128), 16 * bands)
-            pltpu.make_async_copy(
-                total.at[group, m, :], out.at[m, at], out_sem.at[3 * group + tile]
-            ).start()
+            total[xs, m, :] += result
 
         return carry
 
@@ -273,56 +290,82 @@
             wait_round(number - LAG)
         send_round(number)
         exchange(number)
-        count = UNITS.get(number, 0)
+        count = TILES.get(number, 0)
         if count:
             if done == 0:
                 for copy in own_cols:
                     copy.wait()
-            lax.fori_loop(done, done + count, unit, 0)
+            lax.fori_loop(done, done + count, tile, 0)
             done += count
-    for number in range(rounds - LAG, rounds):
+    for number in range(rounds - LAG, rounds - 1):
         wait_round(number)
-    lax.fori_loop(done, 24, unit, 0)
-
-    def flush(u, carry):
-        group, tile = u // 3, u % 3
-        ox = group + (group // 2) * (5 - 2 * group)
-        xs = (x + ox) % NX
-        m = pl.ds(pl.multiple_of(tile * M_TILE, M_TILE), M_TILE)
-        at = pl.ds(pl.multiple_of(xs * 16 * bands, 128), 16 * bands)
-        pltpu.make_async_copy(
-            total.at[group, m, :], out.at[m, at], out_sem.at[3 * group + tile]
-        ).wait()
-        return carry
-
+    lax.fori_loop(done, EARLY, tile, 0)
+    wait_round(rounds - 1)
+    ox, oz = PARTS[-1]
+    fill_right(cols, right_hi, right_lo, (half + oz) % 2, (x + ox) % NX)
     for copy in sends:
         copy.wait_send()
-    lax.fori_loop(0, 12, flush, 0)
+
+
+def last_kernel(left_hi, left_lo, right_hi, right_lo, total, out, result, sems):
+    row, half = lax.axis_index("row"), lax.axis_index("ga")
+    ox, oz = PARTS[-1]
+    xs, h = (row // 4 + ox) % NX, (half + oz) % 2
+    group = result.shape[2]
+
+    def lanes(k):
+        return pl.ds(pl.multiple_of(((xs + k) % NX) * group, 128), group)
+
+    others = []
+    for k in range(1, NX):
+        others.append(pltpu.make_async_copy(
+            total.at[(xs + k) % NX], out.at[:, lanes(k)], sems.at[N_TILE + k - 1]
+        ))
+        others[-1].start()
+
+    def part(m_tile):
+        m = pl.ds(pl.multiple_of(m_tile * M_TILE, M_TILE), M_TILE)
+        return m, pltpu.make_async_copy(
+            result.at[m_tile], out.at[m, lanes(0)], sems.at[m_tile]
+        )
+
+    def tile(m_tile, carry):
+        m, copy = part(m_tile)
+        result[m_tile] = total[xs, m, :] + three(
+            left_hi[h, m, :], left_lo[h, m, :], right_hi[...], right_lo[...]
+        )
+        copy.start()
+        return carry
+
+    lax.fori_loop(0, N_TILE, tile, 0)
+    for m_tile in range(N_TILE):
+        part(m_tile)[1].wait()
+    for copy in others:
+        copy.wait()
 
 
 def local(pair_density, coulomb):
     local_k, bands, width = pair_density.shape
     n_row = lax.axis_size("row")
-    total_k = local_k * n_row
-    scale = jnp.broadcast_to((2.0 * coulomb / F32(total_k))[None, :], (8, width))
     m = 2 * n_row * bands
     n = 4 * n_row * bands
     group = n // NX
     rounds = len(PLAN)
-    return pl.pallas_call(
+    passed = pl.pallas_call(
         kernel,
-        out_shape=jax.ShapeDtypeStruct((m, n), F32),
-        in_specs=[pl.BlockSpec(memory_space=pl.ANY), pl.BlockSpec(memory_space=pltpu.VMEM)],
-        out_specs=pl.BlockSpec(memory_space=pl.ANY),
-        scratch_shapes=[
-            pltpu.VMEM((2, 4 * n_row, bands, width), F32),
-            pltpu.VMEM((2, NY, 2, n_row, bands, width // NY), F32),
-            pltpu.VMEM((2, 8, width), F32),
+        out_shape=[
             pltpu.VMEM((2, m, width), BF16),
             pltpu.VMEM((2, m, width), BF16),
             pltpu.VMEM((group, width), BF16),
             pltpu.VMEM((group, width), BF16),
             pltpu.VMEM((NX, m, group), F32),
+        ],
+        in_specs=[pl.BlockSpec(memory_space=pl.ANY), pl.BlockSpec(memory_space=pltpu.VMEM)],
+        out_specs=[pl.BlockSpec(memory_space=pltpu.VMEM)] * 5,
+        scratch_shapes=[
+            pltpu.VMEM((2, 4 * n_row, bands, width), F32),
+            pltpu.VMEM((2, NY, 2, n_row, bands, width // NY), F32),
+            pltpu.VMEM((2, 8, width), F32),
             pltpu.SemaphoreType.DMA((4 * rounds,)),
             pltpu.SemaphoreType.DMA((4 * rounds,)),
             pltpu.SemaphoreType.DMA((n_row,)),
@@ -330,13 +373,24 @@
             pltpu.SemaphoreType.DMA((16,)),
             pltpu.SemaphoreType.DMA((16,)),
             pltpu.SemaphoreType.DMA((6,)),
-            pltpu.SemaphoreType.DMA((12,)),
         ],
         compiler_params=pltpu.CompilerParams(
-            collective_id=0, has_side_effects=True, vmem_limit_bytes=64 * 1024 * 1024 - 2 * 1024 * 1024
+            collective_id=0, has_side_effects=True, vmem_limit_bytes=FIRST_LIMIT
         ),
         name="gather_and_contract",
-    )(pair_density, scale)
+    )(pair_density, coulomb)
+    return pl.pallas_call(
+        last_kernel,
+        out_shape=jax.ShapeDtypeStruct((m, n), F32),
+        in_specs=[pl.BlockSpec(memory_space=pltpu.VMEM)] * 5,
+        out_specs=pl.BlockSpec(memory_space=pl.ANY),
+        scratch_shapes=[
+            pltpu.VMEM((N_TILE, M_TILE, group), F32),
+            pltpu.SemaphoreType.DMA((N_TILE + NX - 1,)),
+        ],
+        compiler_params=pltpu.CompilerParams(vmem_limit_bytes=LAST_LIMIT),
+        name="contract_last",
+    )(*passed)
 
 
 def solution(mesh):

time: 156 us -> 144 us (0.923)
  Pallas kernels: 150 us -> 143 us
  local copies, waits for them, and re-layouts: 5.47 us -> 0.7 us
    pallas_call x1 -> x2, Pallas kernels: 150 us -> 143 us  [the longest x1 138 us: local(): pl.pallas_call(kernel, out_shape=[pltpu.VMEM((2, m, width), BF16), pltpu....]
    unnamed x1 -> x2, local copies, waits for them, and re-layouts: 4.84 us -> 0.7 us
where the time goes in v2:
time: 144 us
  Pallas kernels  143 us (99%)
    pallas_call x1, Pallas kernels, local(): pl.pallas_call(kernel, out_shape=[pltpu.VMEM((2, m, width), BF16), pltpu....  138 us
    pallas_call x1, Pallas kernels, local(): pl.pallas_call(last_kernel, out_shape=jax.ShapeDtypeStruct((m, n), F32),...  5.09 us

profile of v2, /device:TPU:16, one launch (start us, length us, event | category | flops | bytes accessed | tf_op | source)
XLA Modules:
  0.0 144.0 jit_solution(17358444886651042649)
XLA Ops:
  0.0 0.0 copy-start
  0.0 0.7 copy-done
  0.7 138.2 %gather_and_contract.1 = (bf16[2,768,1536]{2,1,0:T(8,128)(2,1)S(1)}, bf16[2,768,1536]{2,1,0:T(8,128)(2,1)S(1)}, bf16[384,1536]{1,0:T(8,128)(2,1)S(1)}, bf16[384,1536]{1,0:T(8,128)(2,1)S(1)}, f32[4,768,384]{2,1,0:T(8,128)S(1)}) custom-call(f32[32,24,1536]{2,1,0:T(8,128)} %pairs.1, f32[1536]{0:T(1024)S(1)} %copy-done), custom_call_target="tpu_custom_call" | custom-call | tf_op jit(solution)/shard_map/gather_and_contract/pallas_call | solution.py:354
  138.9 5.1 %contract_last.1 = f32[768,1536]{1,0:T(8,128)} custom-call(bf16[2,768,1536]{2,1,0:T(8,128)(2,1)S(1)} %get-tuple-element.10.left_hi, bf16[2,768,1536]{2,1,0:T(8,128)(2,1)S(1)} %get-tuple-element.11.left_lo, bf16[384,1536]{1,0:T(8,128)(2,1)S(1)} %get-tuple-element.12.right_hi, bf16[384,1536]{1,0:T(8,128)(2,1)S(1)} %get-tuple-element.13.right_lo, ...), custom_call_target="tpu_custom_call" | custom-call | tf_op jit(solution)/shard_map/contract_last/pallas_call | solution.py:382
Async XLA Ops:
  0.0 0.7 copy-start

commit v3 on v0

v3 whole, which is shorter than its diff:
```python
import jax
import jax.numpy as jnp
from jax import lax
from jax.experimental import pallas as pl
from jax.experimental.pallas import tpu as pltpu
from jax.sharding import PartitionSpec as P

MESH = pl.DeviceIdType.MESH
F32 = jnp.float32
BF16 = jnp.bfloat16

LAG = 3
PLAN = (
    (1, 1, 2, 2),
    (0, 0, 1, 3),
    (-1, -1, 0, 1),
    (28, 28, 28, 0),
    (4, 5, -1, -1),
    (5, 4, 31, 4),
    (96, 33, 30, 7),
    (100, 37, 3, 5),
    (25, 25, 25, 10),
    (24, 24, -1, -1),
    (9, 9, 26, 11),
    (29, 29, 29, 6),
    (12, 12, 24, 9),
    (20, 20, 23, 13),
    (8, 8, 27, 12),
    (13, 13, 22, 8),
    (17, 17, -1, -1),
    (21, 21, -1, -1),
    (16, 16, -1, -1),
    (121, 61, -1, -1),
    (105, 40, -1, -1),
    (117, 60, -1, -1),
    (109, 44, -1, -1),
    (120, 52, -1, -1),
    (113, 48, -1, -1),
)
STEPS = ((1, 0), (-1, 0), (0, 1), (0, -1))
NX, NZ, NY = 4, 8, 4
M_TILE = 256
FIRST_LIMIT, LAST_LIMIT = 48 * 2**20, 6 * 2**20

CHUNKS = (0, 1, 3, 2)
SEND = (0, 1, 3, 5)
ROWS, PAIR, FIRST, SECOND, RELAY, CORE = 3, 6, 6, 8, 10, 12
SHARED = (1, 3, 2)
N_TILE = 3
CATCH_UP = 19
TILES = {20: 1, 21: 1, 22: 1, 23: 2, 24: 1}


def split(value):
    high = value.astype(BF16)
    return high, (value - high.astype(F32)).astype(BF16)


def contract(left, right):
    return lax.dot_general(
        left, right, (((1,), (1,)), ((), ())), preferred_element_type=F32
    )


def three(left_hi, left_lo, right_hi, right_lo):
    result = contract(left_hi, right_hi)
    result += contract(left_hi, right_lo)
    result += contract(left_lo, right_hi)
    return result


def fill_right(cols, right_hi, right_lo, first, count):
    bands, width = cols.shape[2:]

    def fill(i, carry):
        h, n = i // count, i % count
        hi, lo = split(cols[h, pl.ds(first(n), 2)].reshape(2 * bands, width))
        to = pl.ds(pl.multiple_of(n * 2 * bands, 16), 2 * bands)
        at = pl.ds(pl.multiple_of(h * width, 128), width)
        right_hi[to, at] = hi
        right_lo[to, at] = lo
        return carry

    lax.fori_loop(0, 2 * count, fill, 0)


def merge(shared, total, index, m_tile, xs):
    lane = lax.broadcasted_iota(jnp.int32, (64, 384), 1)
    run = lane // 48
    for i in range(4):
        wide = []
        for owner in range(2):
            one = shared[owner, index, m_tile, 64 * i : 64 * i + 64, :]
            at = 256 + 64 * (i % 2)
            two = shared[owner, index, m_tile, at : at + 64, :]
            if i // 2:
                two = pltpu.roll(two, 64, 1)
            wide.append(jnp.concatenate([one, two, two], axis=1))
        value = wide[0]
        for k in range(1, 8):
            turned = pltpu.roll(wide[k % 2], 48 * ((k + 1) // 2), 1)
            value = jnp.where(run == k, turned, value)
        m = pl.ds(pl.multiple_of(m_tile * M_TILE, M_TILE) + 64 * i, 64)
        total[xs, m, :] = value


def kernel(
    pairs, coulomb, total, shared,
    cols, rows, scales, left_hi, left_lo, right_hi, right_lo,
    col_send, col_recv, row_send, row_recv, sub_send, sub_recv, out_send, out_recv, own_sem,
):
    row, col, half = lax.axis_index("row"), lax.axis_index("col"), lax.axis_index("ga")
    x, y, core = row // 4, col // 2, col % 2
    z = 2 * (row % 4) + half
    other = 1 - half
    width = pairs.shape[2]
    quarter = width // NY
    bands = pairs.shape[1]
    n_row = 16

    def place(xx, zz, cc=None):
        return {"row": 4 * xx + zz // 2, "col": col if cc is None else cc, "ga": zz % 2}

    def near(step):
        return place((x + step[0] + NX) % NX, (z + step[1] + NZ) % NZ)

    y_up = {"row": row, "col": (col + 2) % 8, "ga": half}
    y_down = {"row": row, "col": (col + 6) % 8, "ga": half}
    twin = {"row": row, "col": 2 * y + 1 - core, "ga": half}
    pair = {"row": row, "col": col, "ga": other}

    def remote(src, dst, send, recv, device):
        return pltpu.make_async_remote_copy(
            src_ref=src, dst_ref=dst, send_sem=send, recv_sem=recv,
            device_id=device, device_id_type=MESH,
        )

    zh = row % 4
    sign = 2 * half - 1

    def at_row(xx, zz):
        return 4 * ((xx + NX) % NX) + (zz + 4) % 4

    barrier = pltpu.get_barrier_semaphore()
    peers = [(at_row(x + dx, zh + dz), half) for dx in range(NX) for dz in (-1, 0, 1) if dx or dz]
    peers += [(at_row(x + dx, zh + dz * sign), other) for dx in range(NX) for dz in (1, 2)]
    peers = [{"row": r, "col": col, "ga": g} for r, g in peers] + [pair, y_up, y_down, twin]
    for device in peers:
        pl.semaphore_signal(barrier, inc=1, device_id=device, device_id_type=MESH)

    lanes = pl.ds(pl.multiple_of(y * quarter, 128), quarter)
    own_rows = pltpu.make_async_copy(
        pairs.at[row + 16 * core, :, lanes], rows.at[half, y, core, 4 * x], own_sem.at[0]
    )
    own_rows.start()
    per_row = 2.0 * coulomb[...].reshape(1, width) / F32(pairs.shape[0] * n_row)
    scales[half] = jnp.broadcast_to(per_row, (8, width))
    own_cols = []
    for piece in range(4):
        own_cols.append(pltpu.make_async_copy(
            pairs.at[col + 8 * piece], cols.at[half, 4 * row + piece], own_sem.at[2 + piece]
        ))
        own_cols[-1].start()

    pl.semaphore_wait(barrier, len(peers))

    sends = []

    def go(copy):
        copy.start()
        sends.append(copy)

    def slot(code, step=(0, 0)):
        xs = (x + code // 32 - step[0] + NX) % NX
        zs = (z + (code // 4) % 8 - step[1] + NZ) % NZ
        piece = (2 * half + 2 * (step[1] != 0) + code % 4) % 4
        return zs % 2, 4 * (4 * xs + zs // 2) + piece

    def send_round(number):
        for way, code in enumerate(PLAN[number]):
            if code < 0:
                continue
            where = cols.at[slot(code)]
            src = pairs.at[col + 8 * ((2 * half + code) % 4)] if code < 4 else where
            index = 4 * number + way
            go(remote(src, where, col_send.at[index], col_recv.at[index], near(STEPS[way])))

    def wait_round(number):
        for way, code in enumerate(PLAN[number]):
            if code < 0:
                continue
            where = cols.at[slot(code, STEPS[way])]
            index = 4 * number + way
            remote(
                where, where, col_send.at[index], col_recv.at[index], near(STEPS[way])
            ).wait_recv()

    def part(i, h, yy, cc):
        xs = (x + CHUNKS[i]) % NX
        return rows.at[h, (yy + NY) % NY, cc, pl.ds(4 * xs, 4)]

    def send_part(i, h, yy, number, device):
        ref, at = part(i, h, yy, core), 16 * i + number
        go(remote(ref, ref, sub_send.at[at], sub_recv.at[at], device))

    def wait_part(i, h, yy, cc, number):
        ref, at = part(i, h, yy, cc), 16 * i + number
        remote(ref, ref, sub_send.at[at], sub_recv.at[at], twin).wait_recv()

    def to_twin(i, h, yy, number):
        send_part(i, h, yy, number, twin)

    ways = ((0, 1, 0), (-sign, 1, 1), (sign, 0, 2), (2 * sign, 0, 3))

    def exchange(number):
        for i in range(NX):
            after = number - SEND[i]
            if after == 0:
                for step, same, place_no in ways:
                    if not CHUNKS[i] and place_no == 0:
                        continue
                    to, at = at_row(x - CHUNKS[i], zh + step), 4 * CHUNKS[i] + place_no
                    ga = half if same else other
                    go(remote(
                        pairs.at[to + 16 * core, :, lanes],
                        rows.at[ga, y, core, 4 * x + place_no],
                        row_send.at[at], row_recv.at[at], {"row": to, "col": col, "ga": ga},
                    ))
            if after == ROWS:
                if not CHUNKS[i]:
                    own_rows.wait()
                    go(remote(
                        scales.at[half], scales.at[half], sub_send.at[0], sub_recv.at[0], pair
                    ))
                for place_no in range(4):
                    if not CHUNKS[i] and place_no == 0:
                        continue
                    at = 4 * CHUNKS[i] + place_no
                    where = rows.at[half, y, core, at_row(x + CHUNKS[i], 0) + place_no]
                    remote(where, where, row_send.at[at], row_recv.at[at], pair).wait_recv()
                send_part(i, half, y, 1, pair)
                send_part(i, half, y, 2, y_up)
                send_part(i, half, y, 3, y_down)
                to_twin(i, half, y, 8)
            if after == FIRST:
                wait_part(i, half, y - 1, core, 2)
                send_part(i, half, y - 1, 6, y_up)
                to_twin(i, half, y - 1, 10)
                wait_part(i, half, y + 1, core, 3)
                to_twin(i, half, y + 1, 11)
            if after == PAIR:
                wait_part(i, other, y, core, 1)
                send_part(i, other, y, 4, y_up)
                send_part(i, other, y, 5, y_down)
                to_twin(i, other, y, 9)
            if after == SECOND:
                wait_part(i, other, y + 1, core, 5)
                send_part(i, other, y + 1, 7, y_down)
                to_twin(i, other, y + 1, 12)
                wait_part(i, other, y - 1, core, 4)
                to_twin(i, other, y - 1, 13)
            if after == RELAY:
                wait_part(i, half, y - 2, core, 6)
                to_twin(i, half, y - 2, 14)
                wait_part(i, other, y + 2, core, 7)
                to_twin(i, other, y + 2, 15)
            if after == CORE:
                if not CHUNKS[i]:
                    remote(
                        scales.at[other], scales.at[other], sub_send.at[0], sub_recv.at[0], pair
                    ).wait_recv()
                for n, (h, yy) in enumerate((
                    (half, y), (other, y), (half, y - 1), (half, y + 1),
                    (other, y + 1), (other, y - 1), (half, y - 2), (other, y + 2),
                )):
                    wait_part(i, h, yy, 1 - core, 8 + n)
                fill_left(at_row(x + CHUNKS[i], 0))

    def fill_left(first):
        def fill(i, carry):
            o, yy, n = i // (NY * 4), (i // 4) % NY, i % 4
            h = (o + n // 2) % 2
            r = first + (zh + 4 + (2 * o - 1) * ((n + 1) // 2)) % 4
            at = pl.ds(pl.multiple_of(yy * quarter, 128), quarter)
            both = jnp.concatenate([rows[o, yy, 0, first + n], rows[o, yy, 1, first + n]], axis=0)
            hi, lo = split(both * scales[h, 0:1, at])
            to = pl.ds(pl.multiple_of(r * 2 * bands, 16), 2 * bands)
            at = pl.ds(pl.multiple_of(h * width + yy * quarter, 128), quarter)
            left_hi[to, at] = hi
            left_lo[to, at] = lo
            return carry

        lax.fori_loop(0, 2 * NY * 4, fill, 0)

    def rows_of(m_tile):
        return pl.ds(pl.multiple_of(m_tile * M_TILE, M_TILE), M_TILE)

    def swap(index, m_tile, owner):
        ref = shared.at[owner, index, m_tile]
        at = N_TILE * index + m_tile
        return remote(ref, ref, out_send.at[at], out_recv.at[at], pair)

    def shared_tile(number):
        index, m_tile = number // N_TILE, number % N_TILE
        if m_tile == 0:
            xs = (x + SHARED[index]) % NX
            fill_right(
                cols, right_hi, right_lo, lambda n: 4 * (4 * xs + n) + 2 * half, 4
            )
        m = rows_of(m_tile)
        result = three(
            left_hi[m, :], left_lo[m, :], right_hi[0:256, :], right_lo[0:256, :]
        )
        shared[half, index, m_tile, 0:256, :] = result[:, :128]
        shared[half, index, m_tile, 256:384, :] = result[:128, 128:] + pltpu.roll(
            result[128:, 128:], 64, 1
        )

    def merge_tile(index, m_tile):
        swap(index, m_tile, other).wait_recv()
        merge(shared, total, index, m_tile, (x + SHARED[index]) % NX)

    def merge_offset(index, count):
        def one(m_tile, carry):
            merge_tile(index, m_tile)
            return carry

        lax.fori_loop(0, count, one, 0)

    rounds = len(PLAN)
    zero = jnp.zeros((256 - 8 * bands, 2 * width), BF16)
    right_hi[8 * bands : 256, :] = zero
    right_lo[8 * bands : 256, :] = zero
    waited = sent = done = 0
    for number in range(rounds):
        while waited <= number - (2 if number >= CATCH_UP else LAG):
            wait_round(waited)
            waited += 1
        send_round(number)
        if sent < done:
            swap(sent // N_TILE, sent % N_TILE, half).start()
            sent += 1
        exchange(number)
        for _ in range(TILES.get(number, 0)):
            shared_tile(done)
            done += 1
            if sent < done - 1:
                swap(sent // N_TILE, sent % N_TILE, half).start()
                sent += 1
    for number in range(waited, rounds):
        wait_round(number)
    while done < 3 * N_TILE:
        shared_tile(done)
        done += 1
        swap(sent // N_TILE, sent % N_TILE, half).start()
        sent += 1
    for copy in own_cols:
        copy.wait()
    swap(sent // N_TILE, sent % N_TILE, half).start()
    merge_offset(0, N_TILE)
    fill_right(cols, right_hi, right_lo, lambda n: 16 * x + 2 * n, 8)

    def own_tile(m_tile, carry):
        m = rows_of(m_tile)
        total[x, m, :] = three(left_hi[m, :], left_lo[m, :], right_hi[...], right_lo[...])
        return carry

    lax.fori_loop(0, N_TILE, own_tile, 0)
    merge_offset(1, N_TILE)
    merge_offset(2, N_TILE - 1)
    for copy in sends:
        copy.wait_send()
    for index in range(3):
        for m_tile in range(N_TILE):
            swap(index, m_tile, half).wait_send()
    swap(2, N_TILE - 1, other).wait_recv()


def last_kernel(total, shared, out, result, sems):
    x = lax.axis_index("row") // 4
    group = total.shape[2]

    def lanes(xs):
        return pl.ds(pl.multiple_of(xs * group, 128), group)

    copies = []
    for k in range(NX):
        xs = (x + k) % NX
        for part in range(2):
            m = pl.ds(512 * part, 512 if part == 0 else 256)
            if k == SHARED[2] and part == 1:
                merge(shared, result, 2, N_TILE - 1, 0)
                src = result.at[0, m]
            else:
                src = total.at[xs, m]
            copies.append(pltpu.make_async_copy(
                src, out.at[m, lanes(xs)], sems.at[2 * k + part]
            ))
    last = 2 * SHARED[2] + 1
    for k, copy in enumerate(copies):
        if k != last:
            copy.start()
    copies[last].start()
    for copy in copies:
        copy.wait()


def local(pair_density, coulomb):
    local_k, bands, width = pair_density.shape
    n_row = lax.axis_size("row")
    m = 2 * n_row * bands
    n = 4 * n_row * bands
    group = n // NX
    rounds = len(PLAN)
    passed = pl.pallas_call(
        kernel,
        out_shape=[
            pltpu.VMEM((NX, m, group), F32),
            pltpu.VMEM((2, len(SHARED), N_TILE, m // 2, 128), F32),
        ],
        in_specs=[pl.BlockSpec(memory_space=pl.ANY), pl.BlockSpec(memory_space=pltpu.VMEM)],
        out_specs=[pl.BlockSpec(memory_space=pltpu.VMEM)] * 2,
        scratch_shapes=[
            pltpu.VMEM((2, 4 * n_row, bands, width), F32),
            pltpu.VMEM((2, NY, 2, n_row, bands, width // NY), F32),
            pltpu.VMEM((2, 8, width), F32),
            pltpu.VMEM((m, 2 * width), BF16),
            pltpu.VMEM((m, 2 * width), BF16),
            pltpu.VMEM((group, 2 * width), BF16),
            pltpu.VMEM((group, 2 * width), BF16),
            pltpu.SemaphoreType.DMA((4 * rounds,)),
            pltpu.SemaphoreType.DMA((4 * rounds,)),
            pltpu.SemaphoreType.DMA((n_row,)),
            pltpu.SemaphoreType.DMA((n_row,)),
            pltpu.SemaphoreType.DMA((64,)),
            pltpu.SemaphoreType.DMA((64,)),
            pltpu.SemaphoreType.DMA((3 * N_TILE,)),
            pltpu.SemaphoreType.DMA((3 * N_TILE,)),
            pltpu.SemaphoreType.DMA((6,)),
        ],
        compiler_params=pltpu.CompilerParams(
            collective_id=0, has_side_effects=True, vmem_limit_bytes=FIRST_LIMIT
        ),
        name="gather_and_contract",
    )(pair_density, coulomb)
    return pl.pallas_call(
        last_kernel,
        out_shape=jax.ShapeDtypeStruct((m, n), F32),
        in_specs=[pl.BlockSpec(memory_space=pltpu.VMEM)] * 2,
        out_specs=pl.BlockSpec(memory_space=pl.ANY),
        scratch_shapes=[
            pltpu.VMEM((1, m, group), F32),
            pltpu.SemaphoreType.DMA((2 * NX,)),
        ],
        compiler_params=pltpu.CompilerParams(vmem_limit_bytes=LAST_LIMIT),
        name="write_result",
    )(*passed)


def solution(mesh):
    placed = (P("row", None, "ga"), P("ga"))
    return jax.shard_map(
        local, mesh=mesh, in_specs=placed, out_specs=P("row", "col"), check_vma=False
    )
```

time: 381 us -> 132 us (0.35)
  waiting for transfers between devices: 208 us -> 0 us
  Pallas kernels: 0 us -> 130 us
  blocking collectives: 109 us -> 0 us
  matrix products: 28 us -> 0 us
  other arithmetic: 17.3 us -> 0 us
  between operations: 13.2 us -> 0.17 us
    all_gather x2 -> x0, waiting for transfers between devices: 166 us -> none  [the longest x1 125 us: local(): columns = lax.all_gather(own_columns, 'row', axis=0, tiled=True)]
    pallas_call x0 -> x2, Pallas kernels: none -> 130 us  [the longest x1 128 us: local(): pl.pallas_call(kernel, out_shape=[pltpu.VMEM((NX, m, group), F32), pltpu....]
    all_to_all x1 -> x0, blocking collectives: 109 us -> none  [sent_to_all(): return lax.all_to_all(copies, axis, split_axis=0, concat_axis=0, tiled=True)]
    reduce_scatter x1 -> x0, waiting for transfers between devices: 42.3 us -> none  [from_root(): own = lax.psum_scatter(padded, axis, scatter_dimension=0, tiled=True)]
    dot_general x1 -> x0, matrix products: 28 us -> none  [contract(): lax.dot_general(left_rows, right_rows, (((1,), (1,)), ((), ())), precisio...]
    reduce_sum x1 -> x0, other arithmetic: 7.29 us -> none  [taken_together(): return sent_to_all(value, axis).sum(axis=0)]
    div x1 -> x0, other arithmetic: 4.98 us -> none  [local(): return summed / jnp.float32(total_k)]
    select_n x1 -> x0, other arithmetic: 4.98 us -> none  [from_root(): jnp.where(lax.axis_index(axis) == root, value, jnp.zeros_like(value))]
  transfers between devices with their start and end apart: 3 -> 0, of which waited for: 3 -> 0; matrix products, arithmetic and copies ran while one was open for 0% -> 0% of each run, Pallas kernels for 0% -> 0%
where the time goes in v3:
time: 132 us; the launch traced here: 131 us
  Pallas kernels  130 us (98%)
    pallas_call x1, Pallas kernels, local(): pl.pallas_call(kernel, out_shape=[pltpu.VMEM((NX, m, group), F32), pltpu....  128 us
    pallas_call x1, Pallas kernels, local(): pl.pallas_call(last_kernel, out_shape=jax.ShapeDtypeStruct((m, n), F32),...  2.89 us

profile of v3, /device:TPU:16, one launch (start us, length us, event | category | flops | bytes accessed | tf_op | source)
XLA Modules:
  0.0 130.7 jit_solution(15189770615928536139)
XLA Ops:
  0.0 127.6 %gather_and_contract.1 = (f32[4,768,384]{2,1,0:T(8,128)S(1)}, f32[2,3,3,384,128]{4,3,2,1,0:T(8,128)S(1)}) custom-call(f32[32,24,1536]{2,1,0:T(8,128)} %pairs.1, f32[1536]{0:T(1024)} %coulomb.1), custom_call_target="tpu_custom_call" | custom-call | tf_op jit(solution)/shard_map/gather_and_contract/pallas_call | solution.py:415
  127.6 2.9 %write_result.1 = f32[768,1536]{1,0:T(8,128)} custom-call(f32[4,768,384]{2,1,0:T(8,128)S(1)} %get-tuple-element.7.total, f32[2,3,3,384,128]{4,3,2,1,0:T(8,128)S(1)} %get-tuple-element.8.shared), custom_call_target="tpu_custom_call" | custom-call | tf_op jit(solution)/shard_map/write_result/pallas_call | solution.py:446

commit v4 on v3

--- a/solution.py
+++ b/solution.py
@@ -43,7 +43,7 @@
 FIRST_LIMIT, LAST_LIMIT = 48 * 2**20, 6 * 2**20
 
 CHUNKS = (0, 1, 3, 2)
-SEND = (0, 1, 3, 5)
+SEND = (1, 3, 5, 7)
 ROWS, PAIR, FIRST, SECOND, RELAY, CORE = 3, 6, 6, 8, 10, 12
 SHARED = (1, 3, 2)
 N_TILE = 3

time: 132 us -> 131 us (level)
  no operation moved by 1% of the time
where the time goes in v4:
time: 131 us
  Pallas kernels  130 us (99%)
    pallas_call x1, Pallas kernels, local(): pl.pallas_call(kernel, out_shape=[pltpu.VMEM((NX, m, group), F32), pltpu....  128 us
    pallas_call x1, Pallas kernels, local(): pl.pallas_call(last_kernel, out_shape=jax.ShapeDtypeStruct((m, n), F32),...  2.89 us

profile of v4, /device:TPU:16, one launch (start us, length us, event | category | flops | bytes accessed | tf_op | source)
XLA Modules:
  0.0 130.7 jit_solution(2941381600716551726)
XLA Ops:
  0.0 127.6 %gather_and_contract.1 = (f32[4,768,384]{2,1,0:T(8,128)S(1)}, f32[2,3,3,384,128]{4,3,2,1,0:T(8,128)S(1)}) custom-call(f32[32,24,1536]{2,1,0:T(8,128)} %pairs.1, f32[1536]{0:T(1024)} %coulomb.1), custom_call_target="tpu_custom_call" | custom-call | tf_op jit(solution)/shard_map/gather_and_contract/pallas_call | solution.py:415
  127.6 2.9 %write_result.1 = f32[768,1536]{1,0:T(8,128)} custom-call(f32[4,768,384]{2,1,0:T(8,128)S(1)} %get-tuple-element.7.total, f32[2,3,3,384,128]{4,3,2,1,0:T(8,128)S(1)} %get-tuple-element.8.shared), custom_call_target="tpu_custom_call" | custom-call | tf_op jit(solution)/shard_map/write_result/pallas_call | solution.py:446
